TPU v7x, 32 devices: a whole 2x2x4 slice. The times are simulated.
32 devices in a mesh: island: 16 (over z, y, x), tensor: 2 (over core).
Axes of the slice: x: 2, y: 2, z: 4, core: 2. Of those that a mesh axis runs over, the one named last changes fastest.
Arguments:
- pseudo_grad: float32 [16, 32, 53248], P('island', None, 'tensor'), may hold values from -8000 to 8000
- outer_params: float32 [32, 53248], P('island', 'tensor'), may hold values from -4 to 4
- momentum: float32 [32, 53248], P('island', 'tensor'), may hold values from -6 to 6
- save_pages: int32 [16], replicated, may hold values from 1 to 832, 6656 in all
- writer: int32 [16], replicated, may hold values from 0 to 15, each once
Outputs:
- new_master: float32 [32, 53248], P('island', 'tensor')
- new_momentum: float32 [32, 53248], P('island', 'tensor')
- checkpoint: bfloat16 [16, 832, 256], P('island', None, 'tensor')
Inputs may be any that keep to these rules, and one draw needn't show every extreme that they name: save_pages sums to 6656; the longest range has exactly 832 pages. writer names every island once.
All inputs are finite; a program needn't handle non-finite values.
Results may differ from a plain program's by a relative error of at most 0.0007.
Values may be sent and summed in bfloat16 or wider, within the bound.
A program may use at most 64 MiB of HBM per device.

v0:
```python
import jax
import jax.numpy as jnp
from jax import lax
from jax.sharding import PartitionSpec as P

epsilon = 1e-06
decay_rate = 0.9
outer_rate = 0.7


def body(pseudo_grad, outer_params, momentum, save_pages, writer):
    own_rows = outer_params.shape[0]
    col_width = outer_params.shape[1]
    islands = lax.axis_size("island")
    my_index = lax.axis_index("island")
    own_grad = pseudo_grad[0]
    entries = own_grad.shape[0] * col_width * lax.axis_size("tensor")
    summed = lax.psum(own_grad, "island")
    full_grad = summed / islands
    square_sum = lax.psum(jnp.sum(full_grad * full_grad), "tensor")
    outer_grad = lax.dynamic_slice_in_dim(full_grad, my_index * own_rows, own_rows, 0)
    normed = outer_grad / jnp.sqrt(square_sum / entries + epsilon)
    new_momentum = decay_rate * momentum + normed
    new_master = outer_params - outer_rate * (normed + decay_rate * new_momentum)
    cast_rows = new_master.astype(jnp.bfloat16)
    pages_own = own_rows * col_width // 128
    capacity = 2 * pages_own
    starts = jnp.cumsum(save_pages) - save_pages
    targets = jnp.arange(islands, dtype=jnp.int32)
    owner_table = writer[None, :] == targets[:, None]
    range_start = jnp.sum(jnp.where(owner_table, starts[None, :], 0), axis=1)
    range_length = jnp.sum(jnp.where(owner_table, save_pages[None, :], 0), axis=1)
    is_mine = targets == my_index
    own_start = jnp.sum(jnp.where(is_mine, range_start, 0))
    own_length = jnp.sum(jnp.where(is_mine, range_length, 0))
    slot_ids = jnp.arange(capacity, dtype=jnp.int32)
    own_pages = cast_rows.reshape(pages_own, 128)
    spread_slots = -(-pages_own // islands)
    deliver_slots = -(-capacity // islands)
    spread_ids = jnp.arange(spread_slots, dtype=jnp.int32)
    offset = jnp.mod(targets - my_index * pages_own, islands)
    local_index = offset[:, None] + islands * spread_ids[None, :]
    live_slot = (local_index < pages_own).reshape(-1, 1)
    outgoing = jnp.take(own_pages, jnp.clip(local_index, 0, pages_own - 1).reshape(-1), axis=0)
    outgoing = jnp.where(live_slot, outgoing, jnp.zeros_like(outgoing))
    spread = lax.all_to_all(outgoing, "island", split_axis=0, concat_axis=0, tiled=True)
    deliver_ids = jnp.arange(deliver_slots, dtype=jnp.int32)
    first_page = range_start + jnp.mod(my_index - range_start, islands)
    global_page = first_page[:, None] + islands * deliver_ids[None, :]
    live_out = (global_page < (range_start + range_length)[:, None]).reshape(-1, 1)
    held_index = (
        global_page // pages_own * spread_slots + jnp.mod(global_page, pages_own) // islands
    )
    held_index = jnp.clip(held_index, 0, islands * spread_slots - 1).reshape(-1)
    forward = jnp.take(spread, held_index, axis=0)
    forward = jnp.where(live_out, forward, jnp.zeros_like(forward))
    delivered = lax.all_to_all(forward, "island", split_axis=0, concat_axis=0, tiled=True)
    source = jnp.mod(own_start + slot_ids, islands) * deliver_slots + slot_ids // islands
    source = jnp.clip(source, 0, islands * deliver_slots - 1)
    packed = jnp.take(delivered, source, axis=0)
    packed = jnp.where((slot_ids < own_length)[:, None], packed, jnp.zeros_like(packed))
    return (new_master, new_momentum, packed[None])


def solution(mesh):
    in_specs = (P("island", None, "tensor"), P("island", "tensor"), P("island", "tensor"), P(), P())
    out_specs = (P("island", "tensor"), P("island", "tensor"), P("island", None, "tensor"))
    return jax.shard_map(body, mesh=mesh, in_specs=in_specs, out_specs=out_specs, check_vma=False)
```

profile of v0, /device:TPU:0, one launch (start us, length us, event | category | flops | bytes accessed | tf_op | source)
XLA Modules:
  0.0 218.6 jit_solution(9376555139836277744)
XLA Ops:
  7.2 0.0 all-reduce.2.cloned.1.call-start
  7.2 0.7 all-reduce.2.cloned.1.call-update
  8.0 0.1 add_clamp_fusion
  8.0 0.1 min.40
  8.1 0.1 copy.10
  8.3 0.1 reduce
  8.4 0.1 select_reduce_fusion.1
  8.5 0.7 fusion.32
  9.2 0.1 add_divide_fusion
  9.3 0.1 rem.175
  9.4 0.1 div.75
  9.5 0.1 add_compare_fusion
  9.6 0.1 ne.202
  9.7 0.1 add_compare_fusion.1
  9.8 159.0 %all-reduce.2.cloned.1.call-done = f32[32,26624]{1,0:T(8,128)} async-done(((f32[32,26624]{1,0:T(8,128)}), f32[32,26624]{1,0:T(8,128)}) %all-reduce.2.cloned.1.call-update) | async-done | bytes 3407888 | tf_op jit(solution)/shard_map/psum | solution.py:18
  168.8 3.5 %broadcast_multiply_fusion = (f32[32,26624]{1,0:T(8,128)S(1)}, f32[]{:T(128)}) fusion(f32[32,26624]{1,0:T(8,128)} %all-reduce.2.cloned.1.call-done), kind=kLoop, calls=%fused_computation.4 | loop fusion | flops 2555903 | bytes 6815748 | tf_op jit(solution)/shard_map/div | solution.py:19
  172.2 3.1 %psum.15 = f32[]{:T(128)} all-reduce(f32[]{:T(128)} %get-tuple-element.9), channel_id=1, replica_groups=mesh['island'=16,'tensor'=2] {'tensor'}, use_global_device_ids=true, to_apply=%region_2.0 | all-reduce | flops 1 | bytes 8 | tf_op jit(solution)/shard_map/psum | solution.py:20
  176.0 2.1 fusion.36
  178.1 0.1 reshape.458
  178.2 1.5 gather_fusion
  179.7 0.9 select_select_fusion.1
  180.6 4.7 %all-to-all-start = ((bf16[16,26,128]{2,1,0:T(8,128)(2,1)}), bf16[16,26,128]{2,1,0:T(8,128)(2,1)S(1)}, u32[]{:S(2)}, u32[]{:S(2)}) async-start(bf16[16,26,128]{2,1,0:T(8,128)(2,1)} %select_select_fusion.1), calls=%async_computation | async-start | bytes 262144 | tf_op jit(solution)/shard_map/all_to_all | solution.py:46
  185.3 0.1 fusion.25
  185.4 7.7 %all-to-all-done = bf16[16,26,128]{2,1,0:T(8,128)(2,1)S(1)} async-done(((bf16[16,26,128]{2,1,0:T(8,128)(2,1)}), bf16[16,26,128]{2,1,0:T(8,128)(2,1)S(1)}, u32[]{:S(2)}, u32[]{:S(2)}) %all-to-all-start) | async-done | bytes 106528 | tf_op jit(solution)/shard_map/all_to_all | solution.py:46
  193.1 2.4 %gather_fusion.1 = bf16[832,128]{1,0:T(8,128)(2,1)S(1)} fusion(bf16[416,128]{1,0:T(8,128)(2,1)S(1)} %all_to_all.13, s32[1024]{0:T(1024)S(1)} %pad_clamp_fusion.1), kind=kCustom, calls=%fused_computation.1 | custom fusion | bytes 429312 | tf_op jit(solution)/shard_map/jit(_take)/gather | solution.py:55
  195.5 1.0 select_select_fusion
  196.5 3.5 %all-to-all-start.1 = ((bf16[16,52,128]{2,1,0:T(8,128)(2,1)}), bf16[16,52,128]{2,1,0:T(8,128)(2,1)S(1)}, u32[]{:S(2)}, u32[]{:S(2)}) async-start(bf16[16,52,128]{2,1,0:T(8,128)(2,1)} %select_select_fusion), calls=%async_computation.1 | async-start | bytes 458752 | tf_op jit(solution)/shard_map/all_to_all | solution.py:57
  200.1 0.7 fusion.26
  200.8 1.3 iota_compare_fusion.1
  202.1 6.3 %all-to-all-done.1 = bf16[16,52,128]{2,1,0:T(8,128)(2,1)S(1)} async-done(((bf16[16,52,128]{2,1,0:T(8,128)(2,1)}), bf16[16,52,128]{2,1,0:T(8,128)(2,1)S(1)}, u32[]{:S(2)}, u32[]{:S(2)}) %all-to-all-start.1) | async-done | bytes 213024 | tf_op jit(solution)/shard_map/all_to_all | solution.py:57
  208.4 2.4 %gather_fusion.2 = bf16[832,128]{1,0:T(8,128)(2,1)S(1)} fusion(bf16[832,128]{1,0:T(8,128)(2,1)S(1)} %all_to_all.15, s32[1024]{0:T(1024)S(1)} %pad_clamp_fusion), kind=kCustom, calls=%fused_computation.2 | custom fusion | bytes 429312 | tf_op jit(solution)/shard_map/jit(_take)/gather | solution.py:60
  210.8 1.0 fusion
  (17 shorter events, 0.3 us)
Async XLA Ops:
  7.2 1.0 copy-start
  7.2 1.2 copy-start.1
  7.2 161.6 %all-reduce.2.cloned.1.call-start = ((), (), s32[]{:S(2)}) async-start(), calls=%async_computation.2 | async-start | bytes 6815744 | tf_op jit(solution)/shard_map/psum | solution.py:18
  180.6 12.5 %all-to-all-start = ((bf16[16,26,128]{2,1,0:T(8,128)(2,1)}), bf16[16,26,128]{2,1,0:T(8,128)(2,1)S(1)}, u32[]{:S(2)}, u32[]{:S(2)}) async-start(bf16[16,26,128]{2,1,0:T(8,128)(2,1)} %select_select_fusion.1), calls=%async_computation | async-start | bytes 262144 | tf_op jit(solution)/shard_map/all_to_all | solution.py:46
  196.5 11.8 %all-to-all-start.1 = ((bf16[16,52,128]{2,1,0:T(8,128)(2,1)}), bf16[16,52,128]{2,1,0:T(8,128)(2,1)S(1)}, u32[]{:S(2)}, u32[]{:S(2)}) async-start(bf16[16,52,128]{2,1,0:T(8,128)(2,1)} %select_select_fusion), calls=%async_computation.1 | async-start | bytes 458752 | tf_op jit(solution)/shard_map/all_to_all | solution.py:57
Sparse Core Ops, SparseCore 0:
  13.7 155.0 all-reduce.1
where the time goes:
time: 219 us
  waiting for transfers between devices  174 us (79%)
  between operations  14.9 us (7%)
  other arithmetic  11.8 us (5%)
  starting transfers between devices  8.25 us (4%)
  local copies, waits for them, and re-layouts  6.87 us (3%)
  blocking collectives  3.08 us (1%)
    psum x1, waiting for transfers between devices, body(): summed = lax.psum(own_grad, 'island')  159 us
    all_to_all x1, waiting for transfers between devices, body(): lax.all_to_all(outgoing, 'island', split_axis=0, concat_axis=0, tiled=True)  7.72 us
    all_to_all x1, waiting for transfers between devices, body(): lax.all_to_all(forward, 'island', split_axis=0, concat_axis=0, tiled=True)  6.3 us
    all_to_all x1, starting transfers between devices, body(): lax.all_to_all(outgoing, 'island', split_axis=0, concat_axis=0, tiled=True)  4.69 us
  transfers between devices with their start and end apart: 3, of which 3 were waited for; matrix products, arithmetic and copies ran while one was open for 2% of the time, Pallas kernels for 0%

commit v1 on v0

--- a/solution.py
+++ b/solution.py
@@ -15,7 +15,20 @@
     my_index = lax.axis_index("island")
     own_grad = pseudo_grad[0]
     entries = own_grad.shape[0] * col_width * lax.axis_size("tensor")
-    summed = lax.psum(own_grad, "island")
+
+    def _mark_wall(x_in):
+        axis_name = "island"
+        cores_n = lax.psum(1, axis_name)
+        right_arr, reply = (x_in, 0)
+        while 1 << reply < cores_n:
+            arr_next = lax.ppermute(
+                right_arr, axis_name, tuple(((m, m ^ 1 << reply) for m in range(cores_n)))
+            )
+            right_arr = right_arr + arr_next
+            reply = reply + 1
+        return right_arr
+
+    summed = _mark_wall(own_grad)
     full_grad = summed / islands
     square_sum = lax.psum(jnp.sum(full_grad * full_grad), "tensor")
     outer_grad = lax.dynamic_slice_in_dim(full_grad, my_index * own_rows, own_rows, 0)

time: 219 us -> 424 us (1.94)
  waiting for transfers between devices: 174 us -> 377 us
  between operations: 14.9 us -> 1.51 us
  starting transfers between devices: 8.25 us -> 18.5 us
  other arithmetic: 11.8 us -> 16.7 us
    ppermute x0 -> x4, waiting for transfers between devices: none -> 363 us  [_mark_wall(): lax.ppermute(right_arr, axis_name, tuple(((m, m ^ 1 << reply) for m in ra...]
    psum x1 -> x0, waiting for transfers between devices: 159 us -> none  [body(): summed = lax.psum(own_grad, 'island')]
    ppermute x0 -> x4, starting transfers between devices: none -> 8.82 us  [_mark_wall(): lax.ppermute(right_arr, axis_name, tuple(((m, m ^ 1 << reply) for m in ra...]
    reduce_sum x0 -> x1, other arithmetic: none -> 5.16 us  [body(): square_sum = lax.psum(jnp.sum(full_grad * full_grad), 'tensor')]
  transfers between devices with their start and end apart: 3 -> 6, of which waited for: 3 -> 6; matrix products, arithmetic and copies ran while one was open for 2% -> 1% of each run, Pallas kernels for 0% -> 0%
where the time goes in v1:
time: 424 us; the launch traced here: 423 us
  waiting for transfers between devices  377 us (89%)
  starting transfers between devices  18.5 us (4%)
  other arithmetic  16.7 us (4%)
  local copies, waits for them, and re-layouts  6.87 us (2%)
    ppermute x4, waiting for transfers between devices, _mark_wall(): lax.ppermute(right_arr, axis_name, tuple(((m, m ^ 1 << reply) for m in ra...  363 us
    ppermute x4, starting transfers between devices, _mark_wall(): lax.ppermute(right_arr, axis_name, tuple(((m, m ^ 1 << reply) for m in ra...  8.82 us
  transfers between devices with their start and end apart: 6, of which 6 were waited for; matrix products, arithmetic and copies ran while one was open for 1% of the time, Pallas kernels for 0%

profile of v1, /device:TPU:0, one launch (start us, length us, event | category | flops | bytes accessed | tf_op | source)
XLA Modules:
  0.0 423.4 jit_solution(7514321474841438113)
XLA Ops:
  0.6 3.0 collective-permute-start
  3.7 73.9 %collective-permute-done = f32[32,26624]{1,0:T(8,128)S(1)} collective-permute-done((f32[32,26624]{1,0:T(8,128)}, f32[32,26624]{1,0:T(8,128)S(1)}, u32[]{:S(2)}, u32[]{:S(2)}) %collective-permute-start) | collective-permute-done | bytes 3407904 | tf_op jit(solution)/shard_map/ppermute | solution.py:24
  77.6 2.4 bitcast_add_fusion
  80.0 1.8 collective-permute-start.1
  81.9 73.1 %collective-permute-done.1 = f32[32,26624]{1,0:T(8,128)S(1)} collective-permute-done((f32[32,26624]{1,0:T(8,128)S(1)}, f32[32,26624]{1,0:T(8,128)S(1)}, u32[]{:S(2)}, u32[]{:S(2)}) %collective-permute-start.1) | collective-permute-done | bytes 3407904 | tf_op jit(solution)/shard_map/ppermute | solution.py:24
  155.0 0.3 add.291
  155.3 1.6 collective-permute-start.2
  156.9 72.5 %collective-permute-done.2 = f32[32,26624]{1,0:T(8,128)S(1)} collective-permute-done((f32[32,26624]{1,0:T(8,128)S(1)}, f32[32,26624]{1,0:T(8,128)S(1)}, u32[]{:S(2)}, u32[]{:S(2)}) %collective-permute-start.2) | collective-permute-done | bytes 3407904 | tf_op jit(solution)/shard_map/ppermute | solution.py:24
  229.4 0.3 add.292
  229.8 2.3 collective-permute-start.3
  232.2 0.1 min.40
  232.4 0.1 reduce
  232.6 0.1 select_reduce_fusion.1
  232.7 0.7 fusion.32
  233.4 0.1 add_compare_fusion
  233.5 0.1 ne.202
  234.0 143.1 %collective-permute-done.3 = f32[32,26624]{1,0:T(8,128)} collective-permute-done((f32[32,26624]{1,0:T(8,128)S(1)}, f32[32,26624]{1,0:T(8,128)}, u32[]{:S(2)}, u32[]{:S(2)}) %collective-permute-start.3) | collective-permute-done | bytes 3407904 | tf_op jit(solution)/shard_map/ppermute | solution.py:24
  377.0 5.2 %multiply_reduce_fusion = (f32[]{:T(128)}, f32[32,26624]{1,0:T(8,128)}) fusion(f32[32,26624]{1,0:T(8,128)S(1)} %add.292, f32[32,26624]{1,0:T(8,128)} %collective-permute-done.3), kind=kLoop, calls=%fused_computation.3 | loop fusion | flops 3407871 | bytes 10223620 | tf_op jit(solution)/shard_map/reduce_sum | solution.py:33
  382.2 3.1 psum.7
  386.0 2.3 fusion.36
  388.4 1.5 gather_fusion
  389.9 0.9 select_select_fusion.1
  390.8 6.2 %all-to-all-start = ((bf16[16,26,128]{2,1,0:T(8,128)(2,1)}), bf16[16,26,128]{2,1,0:T(8,128)(2,1)S(1)}, u32[]{:S(2)}, u32[]{:S(2)}) async-start(bf16[16,26,128]{2,1,0:T(8,128)(2,1)} %select_select_fusion.1), calls=%async_computation | async-start | bytes 262144 | tf_op jit(solution)/shard_map/all_to_all | solution.py:59
  397.0 7.7 %all-to-all-done = bf16[16,26,128]{2,1,0:T(8,128)(2,1)S(1)} async-done(((bf16[16,26,128]{2,1,0:T(8,128)(2,1)}), bf16[16,26,128]{2,1,0:T(8,128)(2,1)S(1)}, u32[]{:S(2)}, u32[]{:S(2)}) %all-to-all-start) | async-done | bytes 106528 | tf_op jit(solution)/shard_map/all_to_all | solution.py:59
  404.8 2.4 gather_fusion.1
  407.2 1.0 select_select_fusion
  408.2 3.5 all-to-all-start.1
  411.7 0.6 fusion.26
  412.3 1.3 iota_compare_fusion.1
  413.6 6.4 %all-to-all-done.1 = bf16[16,52,128]{2,1,0:T(8,128)(2,1)S(1)} async-done(((bf16[16,52,128]{2,1,0:T(8,128)(2,1)}), bf16[16,52,128]{2,1,0:T(8,128)(2,1)S(1)}, u32[]{:S(2)}, u32[]{:S(2)}) %all-to-all-start.1) | async-done | bytes 213024 | tf_op jit(solution)/shard_map/all_to_all | solution.py:70
  420.1 2.4 gather_fusion.2
  422.4 1.0 fusion
  (25 shorter events, 0.9 us)
Async XLA Ops:
  0.6 77.0 %collective-permute-start = (f32[32,26624]{1,0:T(8,128)}, f32[32,26624]{1,0:T(8,128)S(1)}, u32[]{:S(2)}, u32[]{:S(2)}) collective-permute-start(f32[32,26624]{1,0:T(8,128)} %bitcast.8), channel_id=1, source_target_pairs={{0,2},{2,0},{4,6},{6,4},{8,10},{10,8},{12,14},{14,12},{16,18},{18,... | collective-permute-start | bytes 10223624 | tf_op jit(solution)/shard_map/ppermute | solution.py:24
  80.0 74.9 %collective-permute-start.1 = (f32[32,26624]{1,0:T(8,128)S(1)}, f32[32,26624]{1,0:T(8,128)S(1)}, u32[]{:S(2)}, u32[]{:S(2)}) collective-permute-start(f32[32,26624]{1,0:T(8,128)S(1)} %bitcast_add_fusion), channel_id=1, source_target_pairs={{0,4},{2,6},{4,0},{6,2},{8,12},{10,14},{12,8},{14,10},{16,20},{18,... | collective-permute-start | bytes 10223624 | tf_op jit(solution)/shard_map/ppermute | solution.py:24
  155.3 77.0 %copy-start = (s32[16]{0:T(128)S(1)}, s32[16]{0:T(128)}, u32[]{:S(2)}) copy-start(s32[16]{0:T(128)} %param.8) | copy-start | bytes 196
  155.3 77.2 %copy-start.1 = (s32[16]{0:T(128)S(1)}, s32[16]{0:T(128)}, u32[]{:S(2)}) copy-start(s32[16]{0:T(128)} %param.9) | copy-start | bytes 196
  155.3 74.1 %collective-permute-start.2 = (f32[32,26624]{1,0:T(8,128)S(1)}, f32[32,26624]{1,0:T(8,128)S(1)}, u32[]{:S(2)}, u32[]{:S(2)}) collective-permute-start(f32[32,26624]{1,0:T(8,128)S(1)} %add.291), channel_id=1, source_target_pairs={{0,8},{2,10},{4,12},{6,14},{8,0},{10,2},{12,4},{14,6},{16,24},{18,... | collective-permute-start | bytes 10223624 | tf_op jit(solution)/shard_map/ppermute | solution.py:24
  229.8 147.3 %collective-permute-start.3 = (f32[32,26624]{1,0:T(8,128)S(1)}, f32[32,26624]{1,0:T(8,128)}, u32[]{:S(2)}, u32[]{:S(2)}) collective-permute-start(f32[32,26624]{1,0:T(8,128)S(1)} %add.292), channel_id=1, source_target_pairs={{0,16},{2,18},{4,20},{6,22},{8,24},{10,26},{12,28},{14,30},{16,0},... | collective-permute-start | bytes 10223624 | tf_op jit(solution)/shard_map/ppermute | solution.py:24
  390.8 14.0 %all-to-all-start = ((bf16[16,26,128]{2,1,0:T(8,128)(2,1)}), bf16[16,26,128]{2,1,0:T(8,128)(2,1)S(1)}, u32[]{:S(2)}, u32[]{:S(2)}) async-start(bf16[16,26,128]{2,1,0:T(8,128)(2,1)} %select_select_fusion.1), calls=%async_computation | async-start | bytes 262144 | tf_op jit(solution)/shard_map/all_to_all | solution.py:59
  408.2 11.8 %all-to-all-start.1 = ((bf16[16,52,128]{2,1,0:T(8,128)(2,1)}), bf16[16,52,128]{2,1,0:T(8,128)(2,1)S(1)}, u32[]{:S(2)}, u32[]{:S(2)}) async-start(bf16[16,52,128]{2,1,0:T(8,128)(2,1)} %select_select_fusion), calls=%async_computation.1 | async-start | bytes 458752 | tf_op jit(solution)/shard_map/all_to_all | solution.py:70
